TPU v7x, 256 devices: a whole 4x4x8 slice. The times are simulated.
256 devices in a mesh: dp: 2 (over z_hi), group: 16 (over x, y), seq: 8 (over z_lo, core).
Axes of the slice: x: 4, y: 4, z: 8 (z_hi: 2, z_lo: 4; z = z_hi * 4 + z_lo), core: 2. Of those that a mesh axis runs over, the one named last changes fastest.
Arguments:
- queries: bfloat16 [2, 4096, 2560], P('dp', 'group', 'seq'), may hold values from -6 to 6
- keys: bfloat16 [2, 4096, 2560], P('dp', 'group', 'seq'), may hold values from -6 to 6
- values: bfloat16 [2, 4096, 2560], P('dp', 'group', 'seq'), may hold values from -6 to 6
- cotangent: bfloat16 [2, 4096, 2560], P('dp', 'group', 'seq'), may hold values from -18 to 18
- level_bias: float32 [3, 40], P(None, 'seq'), may hold values from -3 to 3
- off_mid: int32 [40], P('seq'), may hold values from 0 to 7
- off_far: int32 [40], P('seq'), may hold values from 0 to 63
Outputs:
- attended: bfloat16 [2, 4096, 2560], P('dp', 'group', 'seq')
- query_grad: bfloat16 [2, 4096, 2560], P('dp', 'group', 'seq')
- key_grad: bfloat16 [2, 4096, 2560], P('dp', 'group', 'seq')
- value_grad: bfloat16 [2, 4096, 2560], P('dp', 'group', 'seq')
- bias_grad: float32 [3, 40], replicated
All inputs are finite; a program needn't handle non-finite values.
Results may differ from a plain program's by a relative error of at most 0.04.
Values may be sent and summed in bfloat16 or wider, within the bound.
No kernel may reach another device: no remote copies, remote signals or barrier semaphores. Data moves between devices by JAX's collectives and lax.ppermute only.
A program may use at most 64 MiB of HBM per device.

v0:
```python
import math
import jax
import jax.numpy as jnp
from jax import lax
from jax.sharding import Mesh
from jax.sharding import PartitionSpec as P

HEADS = 40
R_MID = 8
R_FAR = 64
GROUP = ("group_0", "group_1")
SEQ = ("seq_0", "seq_1")
DP_GROUP_SEQ = ("dp", "group_0", "group_1", "seq_0", "seq_1")


def sent_together(arrays, axis, dim, along):
    widths = [a.shape[along] for a in arrays]
    both = jnp.concatenate(arrays, axis=along)
    filled = lax.all_gather(both, axis, axis=dim, tiled=True)
    return tuple(jnp.split(filled, [sum(widths[:k]) for k in range(1, len(widths))], axis=along))


def one_axis_at_a_time(array, axes):
    for axis in axes:
        array = lax.psum(array, axis)
    return array


def split_up(array, dim, count):
    before, after = (array.shape[:dim], array.shape[dim + 1 :])
    return jnp.moveaxis(array.reshape(*before, count, -1, *after), dim, 0)


def sent_and_summed(array, axis, dim):
    count = lax.axis_size(axis)
    pieces = lax.all_to_all(split_up(array, dim, count), axis, 0, 0, tiled=True)
    return jnp.sum(pieces.astype(jnp.float32), axis=0)


def side_by_side(arrays, axis, dim, along):
    ends, at = ([], 0)
    for a in arrays[:-1]:
        at += a.shape[along]
        ends.append(at)
    both = jnp.concatenate(arrays, axis=along)
    return tuple(jnp.split(sent_and_summed(both, axis, dim), ends, axis=along))


def select_rows(source, stride, offsets):
    count = source.shape[0] // stride
    shaped = source.reshape((count, stride) + source.shape[1:])
    picker = offsets.reshape((1, 1, -1) + (1,) * (source.ndim - 2))
    picker = jnp.broadcast_to(picker, (count, 1) + source.shape[1:])
    return jnp.take_along_axis(shaped, picker, axis=1)[:, 0]


def place_rows(source, stride, offsets, filler):
    heads = source.shape[1]
    marked = jnp.arange(stride, dtype=jnp.int32)[:, None] == offsets[None, :]
    marked = marked.reshape((1, stride, heads) + (1,) * (source.ndim - 2))
    spread = jnp.where(marked, source[:, None], jnp.asarray(filler, source.dtype))
    return spread.reshape((source.shape[0] * stride,) + source.shape[1:])


def forward_level(queries, keys, values, visible, scaling):
    scores = jnp.einsum("qhe,khe->hqk", queries, keys, preferred_element_type=jnp.float32) * scaling
    scores = jnp.where(visible[None], scores, -jnp.inf)
    highest = jnp.max(scores, axis=2, keepdims=True)
    log_sum = highest + jnp.log(jnp.sum(jnp.exp(scores - highest), axis=2, keepdims=True))
    weights = jnp.exp(scores - log_sum).astype(jnp.bfloat16)
    outputs = jnp.einsum("hqk,khe->qhe", weights, values, preferred_element_type=jnp.float32)
    return (log_sum[:, :, 0].T, outputs)


def backward_level(
    queries, keys, values, cotangent, visible, log_total, row_delta, bias_row, scaling
):
    scores = jnp.einsum("qhe,khe->hqk", queries, keys, preferred_element_type=jnp.float32) * scaling
    shifted = scores + bias_row[:, None, None] - log_total.T[:, :, None]
    weight = jnp.where(visible[None], jnp.exp(jnp.where(visible[None], shifted, 0.0)), 0.0)
    inner = jnp.einsum("qhe,khe->hqk", cotangent, values, preferred_element_type=jnp.float32)
    dscore = weight * (inner - row_delta.T[:, :, None])
    dscore_low = dscore.astype(jnp.bfloat16)
    weight_low = weight.astype(jnp.bfloat16)
    query_part = jnp.einsum("hqk,khe->qhe", dscore_low, keys, preferred_element_type=jnp.float32)
    key_part = jnp.einsum("hqk,qhe->khe", dscore_low, queries, preferred_element_type=jnp.float32)
    value_part = jnp.einsum(
        "hqk,qhe->khe", weight_low, cotangent, preferred_element_type=jnp.float32
    )
    return (query_part, key_part, value_part)


def causal_forward(queries, keys, values, scaling):
    length = queries.shape[0]
    block_rows = min(128, length)
    lse_parts = []
    out_parts = []
    for first_row in range(0, length, block_rows):
        last_row = first_row + block_rows
        query_place = jnp.arange(first_row, last_row, dtype=jnp.int32)
        key_place = jnp.arange(last_row, dtype=jnp.int32)
        visible = key_place[None, :] <= query_place[:, None]
        block_lse, block_out = forward_level(
            queries[first_row:last_row], keys[:last_row], values[:last_row], visible, scaling
        )
        lse_parts.append(block_lse)
        out_parts.append(block_out)
    return (jnp.concatenate(lse_parts, 0), jnp.concatenate(out_parts, 0))


def causal_backward(queries, keys, values, cotangent, log_total, row_delta, bias_row, scaling):
    length = queries.shape[0]
    block_rows = min(128, length)
    query_parts = []
    key_total = jnp.zeros(keys.shape, jnp.float32)
    value_total = jnp.zeros(values.shape, jnp.float32)
    for first_row in range(0, length, block_rows):
        last_row = first_row + block_rows
        query_place = jnp.arange(first_row, last_row, dtype=jnp.int32)
        key_place = jnp.arange(last_row, dtype=jnp.int32)
        visible = key_place[None, :] <= query_place[:, None]
        part_q, part_k, part_v = backward_level(
            queries[first_row:last_row],
            keys[:last_row],
            values[:last_row],
            cotangent[first_row:last_row],
            visible,
            log_total[first_row:last_row],
            row_delta[first_row:last_row],
            bias_row,
            scaling,
        )
        query_parts.append(part_q)
        padding = ((0, length - last_row), (0, 0), (0, 0))
        key_total = key_total + jnp.pad(part_k, padding)
        value_total = value_total + jnp.pad(part_v, padding)
    return (jnp.concatenate(query_parts, 0), key_total, value_total)


def blocked_forward(queries, keys, values, query_start, scaling, block_rows):
    key_place = jnp.arange(keys.shape[0], dtype=jnp.int32)
    query_place = query_start + jnp.arange(0, block_rows, dtype=jnp.int32)
    visible = key_place[None, :] <= query_place[:, None]
    block_lse, block_out = forward_level(queries, keys, values, visible, scaling)
    return (block_lse, block_out)


def blocked_backward(
    queries,
    keys,
    values,
    cotangent,
    log_total,
    row_delta,
    query_start,
    bias_row,
    scaling,
    block_rows,
):
    key_place = jnp.arange(keys.shape[0], dtype=jnp.int32)
    query_place = query_start + jnp.arange(0, block_rows, dtype=jnp.int32)
    visible = key_place[None, :] <= query_place[:, None]
    part_q, part_k, part_v = backward_level(
        queries, keys, values, cotangent, visible, log_total, row_delta, bias_row, scaling
    )
    return (part_q, part_k, part_v)


def per_device(queries, keys, values, cotangent, level_bias, off_mid, off_far):
    tok_rows = queries.shape[1]
    width = queries.shape[2]
    local_heads = level_bias.shape[1]
    head_size = width // local_heads
    scaling = head_size ** (-0.5)
    shape_rows = (tok_rows, local_heads, head_size)
    query_rows = queries[0].reshape(shape_rows)
    key_rows = keys[0].reshape(shape_rows)
    value_rows = values[0].reshape(shape_rows)
    grad_rows = cotangent[0].reshape(shape_rows)
    group_place = lax.axis_index(GROUP)
    anchor = jnp.zeros((), jnp.int32)
    near_lse, near_out = causal_forward(query_rows, key_rows, value_rows, scaling)
    mid_count = tok_rows // R_MID
    mid_start = group_place * mid_count
    mid_block = min(64, mid_count)
    mid_queries = select_rows(query_rows, R_MID, off_mid)
    mid_keys = select_rows(key_rows, R_MID, off_mid)
    mid_values = select_rows(value_rows, R_MID, off_mid)
    mid_all_keys, mid_all_values = (
        lax.all_gather(mid_keys, GROUP, axis=0, tiled=True),
        lax.all_gather(mid_values, GROUP, axis=0, tiled=True),
    )
    mid_lse, mid_out = blocked_forward(
        mid_queries, mid_all_keys, mid_all_values, mid_start, scaling, mid_block
    )
    far_count = tok_rows // R_FAR
    far_start = group_place * far_count
    far_queries = select_rows(query_rows, R_FAR, off_far)
    far_keys = select_rows(key_rows, R_FAR, off_far)
    far_values = select_rows(value_rows, R_FAR, off_far)
    far_all_keys, far_all_values = sent_together((far_keys, far_values), GROUP, 0, 1)
    far_lse, far_out = blocked_forward(
        far_queries, far_all_keys, far_all_values, far_start, scaling, far_count
    )
    gate_near = near_lse + level_bias[0][None, :]
    gate_mid = place_rows(mid_lse, R_MID, off_mid, -jnp.inf) + level_bias[1][None, :]
    gate_far = place_rows(far_lse, R_FAR, off_far, -jnp.inf) + level_bias[2][None, :]
    highest = jnp.maximum(gate_near, jnp.maximum(gate_mid, gate_far))
    log_total = highest + jnp.log(
        jnp.exp(gate_near - highest) + jnp.exp(gate_mid - highest) + jnp.exp(gate_far - highest)
    )
    share_near = jnp.exp(gate_near - log_total)
    share_mid = jnp.exp(gate_mid - log_total)
    share_far = jnp.exp(gate_far - log_total)
    mid_full = place_rows(mid_out, R_MID, off_mid, 0.0)
    far_full = place_rows(far_out, R_FAR, off_far, 0.0)
    mixed = (
        share_near[..., None] * near_out
        + share_mid[..., None] * mid_full
        + share_far[..., None] * far_full
    )
    attended = mixed.astype(jnp.bfloat16)
    grad_float = grad_rows.astype(jnp.float32)
    row_delta = jnp.sum(grad_float * attended.astype(jnp.float32), axis=2)
    level_terms = jnp.stack(
        [
            jnp.sum(share_near * (jnp.sum(grad_float * near_out, axis=2) - row_delta), axis=0),
            jnp.sum(share_mid * (jnp.sum(grad_float * mid_full, axis=2) - row_delta), axis=0),
            jnp.sum(share_far * (jnp.sum(grad_float * far_full, axis=2) - row_delta), axis=0),
        ]
    )
    placed_terms = lax.dynamic_update_slice(
        jnp.zeros((3, HEADS), jnp.float32), level_terms, (anchor, lax.axis_index(SEQ) * local_heads)
    )
    bias_total = one_axis_at_a_time(placed_terms, DP_GROUP_SEQ)
    near_dq, near_dk, near_dv = causal_backward(
        query_rows, key_rows, value_rows, grad_rows, log_total, row_delta, level_bias[0], scaling
    )
    mid_grads = select_rows(grad_rows, R_MID, off_mid)
    mid_total = select_rows(log_total, R_MID, off_mid)
    mid_delta = select_rows(row_delta, R_MID, off_mid)
    mid_dq, mid_dk_terms, mid_dv_terms = blocked_backward(
        mid_queries,
        mid_all_keys,
        mid_all_values,
        mid_grads,
        mid_total,
        mid_delta,
        mid_start,
        level_bias[1],
        scaling,
        mid_block,
    )
    mid_dk, mid_dv = side_by_side(
        (mid_dk_terms.astype(jnp.bfloat16), mid_dv_terms.astype(jnp.bfloat16)), GROUP, 0, 1
    )
    far_grads = select_rows(grad_rows, R_FAR, off_far)
    far_total = select_rows(log_total, R_FAR, off_far)
    far_delta = select_rows(row_delta, R_FAR, off_far)
    far_dq, far_dk_terms, far_dv_terms = blocked_backward(
        far_queries,
        far_all_keys,
        far_all_values,
        far_grads,
        far_total,
        far_delta,
        far_start,
        level_bias[2],
        scaling,
        far_count,
    )
    far_dk, far_dv = side_by_side(
        (far_dk_terms.astype(jnp.bfloat16), far_dv_terms.astype(jnp.bfloat16)), GROUP, 0, 1
    )
    query_grad = scaling * (
        near_dq + place_rows(mid_dq, R_MID, off_mid, 0.0) + place_rows(far_dq, R_FAR, off_far, 0.0)
    )
    key_grad = scaling * (
        near_dk + place_rows(mid_dk, R_MID, off_mid, 0.0) + place_rows(far_dk, R_FAR, off_far, 0.0)
    )
    value_grad = (
        near_dv + place_rows(mid_dv, R_MID, off_mid, 0.0) + place_rows(far_dv, R_FAR, off_far, 0.0)
    )
    bias_grad = bias_total / math.sqrt(lax.axis_size("dp") * lax.axis_size(GROUP) * tok_rows)
    out_shape = (1, tok_rows, width)
    return (
        attended.reshape(out_shape),
        query_grad.astype(jnp.bfloat16).reshape(out_shape),
        key_grad.astype(jnp.bfloat16).reshape(out_shape),
        value_grad.astype(jnp.bfloat16).reshape(out_shape),
        bias_grad,
    )


def solution(mesh):
    finer = Mesh(
        mesh.devices.reshape(mesh.shape["dp"], 4, 4, 4, 2),
        ("dp", "group_0", "group_1", "seq_0", "seq_1"),
    )
    in_specs = (
        P("dp", GROUP, SEQ),
        P("dp", GROUP, SEQ),
        P("dp", GROUP, SEQ),
        P("dp", GROUP, SEQ),
        P(None, SEQ),
        P(SEQ),
        P(SEQ),
    )
    out_specs = (
        P("dp", GROUP, SEQ),
        P("dp", GROUP, SEQ),
        P("dp", GROUP, SEQ),
        P("dp", GROUP, SEQ),
        P(),
    )
    return jax.shard_map(
        per_device, mesh=finer, in_specs=in_specs, out_specs=out_specs, check_vma=False
    )
```

profile of v0, /device:TPU:8, one launch (start us, length us, event | category | flops | bytes accessed | tf_op | source)
XLA Modules:
  0.0 704.0 jit_solution(6368570354909001349)
XLA Ops:
  3.4 1.1 reshape_reshape_squeeze.26
  4.5 1.1 copy.273
  5.6 1.2 reshape_reshape_squeeze.27
  10.2 13.7 %gather_fusion.2 = bf16[1280]{0:T(1024)(128)(2,1)S(1)} fusion(bf16[4,64,5,64]{1,0,3,2:T(4,128)(2,1)S(1)} %reshape_reshape_squeeze.26, s32[1280]{0:T(1024)S(1)} %reshape.1163), kind=kCustom, calls=%fused_computation.1.clone | custom fusion | bytes 25600 | tf_op jit(solution)/shard_map/jit(take_along_axis)/gather | solution.py:54
  23.9 13.7 %gather_fusion.3 = bf16[1280]{0:T(1024)(128)(2,1)S(1)} fusion(bf16[4,64,5,64]{1,0,3,2:T(4,128)(2,1)S(1)} %reshape_reshape_squeeze.27, s32[1280]{0:T(1024)S(1)} %reshape.1163), kind=kCustom, calls=%fused_computation.7.clone | custom fusion | bytes 25600 | tf_op jit(solution)/shard_map/jit(take_along_axis)/gather | solution.py:54
  37.7 13.7 %gather_fusion.4 = bf16[1280]{0:T(1024)(128)(2,1)S(1)} fusion(bf16[4,64,5,64]{1,0,3,2:T(4,128)(2,1)S(1)} %reshape_reshape_squeeze.28, s32[1280]{0:T(1024)S(1)} %reshape.1163), kind=kCustom, calls=%fused_computation.8.clone | custom fusion | bytes 25600 | tf_op jit(solution)/shard_map/jit(take_along_axis)/gather | solution.py:54
  51.5 13.7 %gather_fusion.10 = bf16[1280]{0:T(1024)(128)(2,1)S(1)} fusion(bf16[4,64,5,64]{1,0,3,2:T(4,128)(2,1)S(1)} %reshape_reshape_squeeze.31, s32[1280]{0:T(1024)S(1)} %reshape.1163), kind=kCustom, calls=%fused_computation.9.clone | custom fusion | bytes 25600 | tf_op jit(solution)/shard_map/jit(take_along_axis)/gather | solution.py:54
  65.9 23.7 %all_gather.10 = bf16[64,10,64]{2,1,0:T(8,128)(2,1)S(1)} all-gather(bf16[4,10,64]{2,1,0:T(8,128)(2,1)S(1)} %pad_maximum_fusion.3), channel_id=1, replica_groups=mesh['dp'=2,'group_0'=4,'group_1'=4,'seq_0'=4,'seq_1'=2] {'group_0','gro..., dimensions={0}, use_global_device_ids=true | all-gather | bytes 87040 | tf_op jit(solution)/shard_map/all_gather | solution.py:19
  91.6 105.5 %gather_fusion = bf16[10240]{0:T(1024)(128)(2,1)S(1)} fusion(bf16[32,8,5,64]{3,2,1,0:T(8,128)(2,1)S(1)} %reshape_reshape_squeeze.24, s32[10240]{0:T(1024)S(1)} %reshape.1151), kind=kCustom, calls=%fused_computation.clone | custom fusion | bytes 204800 | tf_op jit(solution)/shard_map/jit(take_along_axis)/gather | solution.py:54
  197.4 105.5 %gather_fusion.1 = bf16[10240]{0:T(1024)(128)(2,1)S(1)} fusion(bf16[32,8,5,64]{3,2,1,0:T(8,128)(2,1)S(1)} %reshape_reshape_squeeze.25, s32[10240]{0:T(1024)S(1)} %reshape.1151), kind=kCustom, calls=%fused_computation.4.clone | custom fusion | bytes 204800 | tf_op jit(solution)/shard_map/jit(take_along_axis)/gather | solution.py:54
  303.3 105.5 %gather_fusion.5 = bf16[10240]{0:T(1024)(128)(2,1)S(1)} fusion(bf16[32,8,5,64]{3,2,1,0:T(8,128)(2,1)S(1)} %reshape_reshape_squeeze.29, s32[10240]{0:T(1024)S(1)} %reshape.1151), kind=kCustom, calls=%fused_computation.5.clone | custom fusion | bytes 204800 | tf_op jit(solution)/shard_map/jit(take_along_axis)/gather | solution.py:54
  409.1 105.5 %gather_fusion.7 = bf16[10240]{0:T(1024)(128)(2,1)S(1)} fusion(bf16[32,8,5,64]{3,2,1,0:T(8,128)(2,1)S(1)} %reshape_reshape_squeeze.30, s32[10240]{0:T(1024)S(1)} %reshape.1151), kind=kCustom, calls=%fused_computation.6.clone | custom fusion | bytes 204800 | tf_op jit(solution)/shard_map/jit(take_along_axis)/gather | solution.py:54
  515.5 22.6 %all-gather = bf16[512,1,5,64]{3,0,2,1:T(8,128)(2,1)S(1)} all-gather(bf16[32,1,5,64]{3,0,2,1:T(8,128)(2,1)S(1)} %copy.275), channel_id=2, replica_groups=mesh['dp'=2,'group_0'=4,'group_1'=4,'seq_0'=4,'seq_1'=2] {'group_0','gro..., dimensions={0}, use_global_device_ids=true | all-gather | bytes 348160 | tf_op jit(solution)/shard_map/all_gather | solution.py:190
  542.7 1.1 broadcast_in_dim.438
  543.8 23.1 %all-gather.1 = bf16[512,1,5,64]{3,0,2,1:T(8,128)(2,1)S(1)} all-gather(bf16[32,1,5,64]{3,0,2,1:T(8,128)(2,1)S(1)} %copy.286), channel_id=3, replica_groups=mesh['dp'=2,'group_0'=4,'group_1'=4,'seq_0'=4,'seq_1'=2] {'group_0','gro..., dimensions={0}, use_global_device_ids=true | all-gather | bytes 348160 | tf_op jit(solution)/shard_map/all_gather | solution.py:191
  569.5 2.0 copy.296
  571.5 1.9 fusion.37
  573.4 1.8 fusion.49
  575.6 1.5 fusion.35
  577.1 1.6 multiply_reduce_fusion.2
  585.6 1.1 fusion.20
  588.0 1.7 copy.328
  589.7 1.6 copy.392
  591.3 1.7 reshape.1221
  593.0 5.6 all-to-all-start.1
  601.0 2.2 gather_fusion.6
  603.4 2.7 gather_fusion.8
  607.6 1.2 fusion.8
  608.8 1.3 fusion.16
  610.1 1.2 fusion.7
  614.4 1.1 broadcast_in_dim.434
  617.4 1.7 reshape.1223
  627.7 1.8 copy.283
  630.3 1.3 broadcast_in_dim.431
  631.7 1.1 copy.293
  632.8 1.3 broadcast_in_dim.426
  634.1 1.7 copy.289
  635.8 2.3 fusion.31
  638.4 10.2 %psum.35 = f32[3,40]{1,0:T(4,128)S(1)} all-reduce(f32[3,40]{1,0:T(4,128)S(1)} %dynamic_update_slice.3), channel_id=1, replica_groups=mesh['dp'=2,'group_0'=4,'group_1'=4,'seq_0'=4,'seq_1'=2] {'dp'}, use_global_device_ids=true, to_apply=%region_17.22 | all-reduce | flops 120 | bytes 960 | tf_op jit(solution)/shard_map/psum | solution.py:25
  648.6 10.4 %psum.36 = f32[3,40]{1,0:T(4,128)S(1)} all-reduce(f32[3,40]{1,0:T(4,128)S(1)} %psum.35), channel_id=1, replica_groups=mesh['dp'=2,'group_0'=4,'group_1'=4,'seq_0'=4,'seq_1'=2] {'group_0'}, use_global_device_ids=true, to_apply=%region_18.23 | all-reduce | flops 120 | bytes 960 | tf_op jit(solution)/shard_map/psum | solution.py:25
  659.0 8.6 %psum.37 = f32[3,40]{1,0:T(4,128)S(1)} all-reduce(f32[3,40]{1,0:T(4,128)S(1)} %psum.36), channel_id=1, replica_groups=mesh['dp'=2,'group_0'=4,'group_1'=4,'seq_0'=4,'seq_1'=2] {'group_1'}, use_global_device_ids=true, to_apply=%region_19.24 | all-reduce | flops 120 | bytes 960 | tf_op jit(solution)/shard_map/psum | solution.py:25
  667.5 11.7 %psum.38 = f32[3,40]{1,0:T(4,128)S(1)} all-reduce(f32[3,40]{1,0:T(4,128)S(1)} %psum.37), channel_id=1, replica_groups=mesh['dp'=2,'group_0'=4,'group_1'=4,'seq_0'=4,'seq_1'=2] {'seq_0'}, use_global_device_ids=true, to_apply=%region_20.25 | all-reduce | flops 120 | bytes 960 | tf_op jit(solution)/shard_map/psum | solution.py:25
  679.2 2.5 psum.39
  681.7 5.8 all-to-all-start
  690.6 1.0 reshape.1222
  692.3 1.1 broadcast_in_dim.461
  694.3 5.4 all-to-all-done
  702.0 1.0 fusion.14
  (384 shorter events, 51.9 us)
Async XLA Ops:
  0.6 6.1 copy-start
  0.6 6.3 copy-start.6
  0.7 6.7 copy-start.4
  1.4 63.8 %copy-start.81 = (s32[5]{0:T(128)}, s32[5]{0:T(128)S(1)}, u32[]{:S(2)}) copy-start(s32[5]{0:T(128)S(1)} %broadcast_add_fusion) | copy-start | bytes 64
  2.0 63.2 %copy-start.83 = (pred[5]{0:T(512)(128)(4,1)}, pred[5]{0:T(512)(128)(4,1)S(1)}, u32[]{:S(2)}) copy-start(pred[5]{0:T(512)(128)(4,1)S(1)} %broadcast_compare_fusion) | copy-start | bytes 19
  2.7 512.0 %copy-start.75 = (s32[5]{0:T(128)}, s32[5]{0:T(128)S(1)}, u32[]{:S(2)}) copy-start(s32[5]{0:T(128)S(1)} %broadcast_add_fusion.1) | copy-start | bytes 64
  3.4 511.4 %copy-start.77 = (pred[5]{0:T(512)(128)(4,1)}, pred[5]{0:T(512)(128)(4,1)S(1)}, u32[]{:S(2)}) copy-start(pred[5]{0:T(512)(128)(4,1)S(1)} %broadcast_compare_fusion.1) | copy-start | bytes 19
  7.7 532.2 %copy-start.20 = (bf16[1,128,320]{1,2,0:T(8,128)(2,1)}, bf16[1,128,320]{1,2,0:T(8,128)(2,1)S(1)}, u32[]{:S(2)}) copy-start(bf16[1,128,320]{1,2,0:T(8,128)(2,1)S(1)} %get-tuple-element.51) | copy-start | bytes 245764
  7.8 604.5 %copy-start.32 = (pred[128,128]{0,1:T(8,128)(4,1)}, pred[128,128]{0,1:T(8,128)(4,1)S(1)}, u32[]{:S(2)}) copy-start(pred[128,128]{0,1:T(8,128)(4,1)S(1)} %iota_compare_fusion.2) | copy-start | bytes 49156
  7.8 532.1 %copy-start.22 = (bf16[1,128,320]{1,2,0:T(8,128)(2,1)}, bf16[1,128,320]{1,2,0:T(8,128)(2,1)S(1)}, u32[]{:S(2)}) copy-start(bf16[1,128,320]{1,2,0:T(8,128)(2,1)S(1)} %slice.66) | copy-start | bytes 245764
  9.3 532.0 %copy-start.40 = (pred[256,5]{0,1:T(8,128)(4,1)}, pred[256,5]{0,1:T(8,128)(4,1)S(1)}, u32[]{:S(2)}) copy-start(pred[256,5]{0,1:T(8,128)(4,1)S(1)} %broadcast_in_dim.420) | copy-start | bytes 3844
  65.9 25.4 %copy-start.64 = (bf16[4,5,64]{2,1,0:T(8,128)(2,1)}, bf16[4,5,64]{2,1,0:T(8,128)(2,1)S(1)}, u32[]{:S(2)}) copy-start(bf16[4,5,64]{2,1,0:T(8,128)(2,1)S(1)} %get-tuple-element.78) | copy-start | bytes 7684
  90.4 451.5 %copy-start.99 = (pred[4,64]{1,0:T(4,128)(4,1)}, pred[4,64]{1,0:T(4,128)(4,1)S(1)}, u32[]{:S(2)}) copy-start(pred[4,64]{1,0:T(4,128)(4,1)S(1)} %iota_compare_fusion.5) | copy-start | bytes 772
  90.6 451.3 %copy-start.57 = (f32[5,4,64]{2,1,0:T(4,128)}, f32[5,4,64]{2,1,0:T(4,128)S(1)}, u32[]{:S(2)}) copy-start(f32[5,4,64]{2,1,0:T(4,128)S(1)} %get-tuple-element.82) | copy-start | bytes 15364
  90.8 451.1 %copy-start.54 = (f32[5,4]{1,0:T(8,128)}, f32[5,4]{1,0:T(8,128)S(1)}, u32[]{:S(2)}) copy-start(f32[5,4]{1,0:T(8,128)S(1)} %log_add_fusion.4) | copy-start | bytes 244
  515.5 23.4 %copy-start.28 = (bf16[32,5,64]{2,1,0:T(8,128)(2,1)}, bf16[32,5,64]{2,1,0:T(8,128)(2,1)S(1)}, u32[]{:S(2)}) copy-start(bf16[32,5,64]{2,1,0:T(8,128)(2,1)S(1)} %get-tuple-element.70) | copy-start | bytes 61444
  539.9 3.9 copy-start.38
  540.2 33.3 %copy-start.1 = (f32[5,128,128]{1,2,0:T(8,128)}, f32[5,128,128]{1,2,0:T(8,128)S(1)}, u32[]{:S(2)}) copy-start(f32[5,128,128]{1,2,0:T(8,128)S(1)} %get-tuple-element.86) | copy-start | bytes 983044
  571.5 3.7 copy-start.55
  575.2 6.5 copy-start.56
  575.2 6.5 copy-start.60
  575.2 6.5 copy-start.62
  575.2 6.5 copy-start.68
  575.2 6.5 copy-start.89
  582.8 3.9 copy-start.65
  583.8 14.9 %copy-start.74 = (s32[5]{0:T(128)S(1)}, s32[5]{0:T(128)}, u32[]{:S(2)}) copy-start(s32[5]{0:T(128)} %param.20) | copy-start | bytes 64
  583.8 14.9 %copy-start.76 = (s32[5]{0:T(128)S(1)}, s32[5]{0:T(128)}, u32[]{:S(2)}) copy-start(s32[5]{0:T(128)} %copy-done.75) | copy-start | bytes 64
  583.8 15.6 %copy-start.51 = (f32[256,5]{0,1:T(8,128)S(1)}, f32[256,5]{0,1:T(8,128)}, u32[]{:S(2)}) copy-start(f32[256,5]{0,1:T(8,128)} %copy-done.50) | copy-start | bytes 15364
  583.8 16.3 %copy-start.5 = (bf16[1,256,320]{1,2,0:T(8,128)(2,1)S(1)}, bf16[1,256,320]{1,2,0:T(8,128)(2,1)}, u32[]{:S(2)}) copy-start(bf16[1,256,320]{1,2,0:T(8,128)(2,1)} %param.18) | copy-start | bytes 491524
  593.0 88.6 %all-to-all-start.1 = ((bf16[16,2,1280]{2,1,0:T(2,128)(2,1)}), bf16[16,2,1280]{2,1,0:T(2,128)(2,1)}, u32[]{:S(2)}, u32[]{:S(2)}) async-start(bf16[16,2,1280]{2,1,0:T(2,128)(2,1)} %reshape.1221), calls=%async_computation.1 | async-start | bytes 163840 | tf_op jit(solution)/shard_map/all_to_all | solution.py:36
  608.8 3.5 copy-start.2
  608.8 3.5 copy-start.29
  608.8 3.5 copy-start.44
  608.8 3.5 copy-start.69
  608.8 3.5 copy-start.92
  608.8 3.5 copy-start.95
  625.7 3.8 copy-start.10
  627.7 8.1 %copy-start.8 = (f32[1,256,320]{2,1,0:T(8,128)S(1)}, f32[1,256,320]{2,1,0:T(8,128)}, u32[]{:S(2)}) copy-start(f32[1,256,320]{2,1,0:T(8,128)} %copy.290) | copy-start | bytes 983044
  627.7 8.1 %copy-start.9 = (f32[1,256,320]{2,1,0:T(8,128)S(1)}, f32[1,256,320]{2,1,0:T(8,128)}, u32[]{:S(2)}) copy-start(f32[1,256,320]{2,1,0:T(8,128)} %copy.294) | copy-start | bytes 983044
  627.7 8.1 %copy-start.17 = (f32[1,128,320]{2,1,0:T(8,128)S(1)}, f32[1,128,320]{2,1,0:T(8,128)}, u32[]{:S(2)}) copy-start(f32[1,128,320]{2,1,0:T(8,128)} %copy.299) | copy-start | bytes 491524
  638.1 49.9 %copy-start.16 = (bf16[1,256,320]{2,1,0:T(8,128)(2,1)S(1)}, bf16[1,256,320]{2,1,0:T(8,128)(2,1)}, u32[]{:S(2)}) copy-start(bf16[1,256,320]{2,1,0:T(8,128)(2,1)} %get-tuple-element.46) | copy-start | bytes 491524
  638.1 50.7 %copy-start.15 = (bf16[1,256,320]{2,1,0:T(8,128)(2,1)S(1)}, bf16[1,256,320]{2,1,0:T(8,128)(2,1)}, u32[]{:S(2)}) copy-start(bf16[1,256,320]{2,1,0:T(8,128)(2,1)} %get-tuple-element.45) | copy-start | bytes 491524
  638.1 51.5 %copy-start.3 = (f32[5,128,128]{1,2,0:T(8,128)S(1)}, f32[5,128,128]{1,2,0:T(8,128)}, u32[]{:S(2)}) copy-start(f32[5,128,128]{1,2,0:T(8,128)} %copy-done.1) | copy-start | bytes 983044
  638.1 51.5 %copy-start.33 = (pred[128,128]{0,1:T(8,128)(4,1)S(1)}, pred[128,128]{0,1:T(8,128)(4,1)}, u32[]{:S(2)}) copy-start(pred[128,128]{0,1:T(8,128)(4,1)} %copy-done.32) | copy-start | bytes 49156
  638.1 51.5 %copy-start.45 = (bf16[1,128,320]{1,2,0:T(8,128)(2,1)S(1)}, bf16[1,128,320]{1,2,0:T(8,128)(2,1)}, u32[]{:S(2)}) copy-start(bf16[1,128,320]{1,2,0:T(8,128)(2,1)} %get-tuple-element.49) | copy-start | bytes 245764
  638.1 51.5 %copy-start.71 = (f32[5]{0:T(128)S(1)}, f32[5]{0:T(128)}, u32[]{:S(2)}) copy-start(f32[5]{0:T(128)} %copy-done.67) | copy-start | bytes 64
  638.1 51.5 %copy-start.93 = (f32[5,128]{1,0:T(8,128)S(1)}, f32[5,128]{1,0:T(8,128)}, u32[]{:S(2)}) copy-start(f32[5,128]{1,0:T(8,128)} %get-tuple-element.88) | copy-start | bytes 7684
  681.7 18.1 %all-to-all-start = ((bf16[16,2,10240]{2,1,0:T(2,128)(2,1)}), bf16[16,2,10240]{2,1,0:T(2,128)(2,1)S(1)}, u32[]{:S(2)}, u32[]{:S(2)}) async-start(bf16[16,2,10240]{2,1,0:T(2,128)(2,1)} %reshape.1223), calls=%async_computation | async-start | bytes 1310720 | tf_op jit(solution)/shard_map/all_to_all | solution.py:36
  (56 other events, 100.3 us)
where the time goes:
time: 705 us; the launch traced here: 704 us
  local copies, waits for them, and re-layouts  537 us (76%)
  blocking collectives  113 us (16%)
  matrix products  18.4 us (3%)
  other arithmetic  17 us (2%)
  starting transfers between devices  11.3 us (2%)
    gather x29, local copies, waits for them, and re-layouts, select_rows(): return jnp.take_along_axis(shaped, picker, axis=1)[:, 0]  485 us
    psum x5, blocking collectives, one_axis_at_a_time(): array = lax.psum(array, axis)  43.3 us
    all_gather x1, blocking collectives, sent_together(): filled = lax.all_gather(both, axis, axis=dim, tiled=True)  23.7 us
    all_gather x1, blocking collectives, per_device(): lax.all_gather(mid_values, GROUP, axis=0, tiled=True)  23.1 us
    all_gather x1, blocking collectives, per_device(): lax.all_gather(mid_keys, GROUP, axis=0, tiled=True)  22.6 us
    broadcast_in_dim x38, local copies, waits for them, and re-layouts, place_rows(): jnp.where(marked, source[:, None], jnp.asarray(filler, source.dtype))  20.4 us
  transfers between devices with their start and end apart: 2, of which 1 were waited for; matrix products, arithmetic and copies ran while one was open for 6% of the time, Pallas kernels for 0%

commit v1 on v0

--- a/solution.py
+++ b/solution.py
@@ -187,7 +187,9 @@
     mid_keys = select_rows(key_rows, R_MID, off_mid)
     mid_values = select_rows(value_rows, R_MID, off_mid)
     mid_all_keys, mid_all_values = (
-        lax.all_gather(mid_keys, GROUP, axis=0, tiled=True),
+        jnp.concatenate(
+            lax.all_to_all(jnp.stack([mid_keys] * lax.axis_size(GROUP)), GROUP, 0, 0), axis=0
+        ),
         lax.all_gather(mid_values, GROUP, axis=0, tiled=True),
     )
     mid_lse, mid_out = blocked_forward(

time: 705 us -> 666 us (0.945)
  blocking collectives: 113 us -> 89.6 us
  local copies, waits for them, and re-layouts: 537 us -> 523 us
  starting transfers between devices: 11.3 us -> 19.2 us
    all_gather x1 -> x0, blocking collectives: 22.6 us -> none  [per_device(): lax.all_gather(mid_keys, GROUP, axis=0, tiled=True)]
    all_to_all x0 -> x1, starting transfers between devices: none -> 7.39 us  [per_device(): lax.all_to_all(jnp.stack([mid_keys] * lax.axis_size(GROUP)), GROUP, 0, 0)]
  transfers between devices with their start and end apart: 2 -> 3, of which waited for: 1 -> 1; matrix products, arithmetic and copies ran while one was open for 6% -> 13% of each run, Pallas kernels for 0% -> 0%
where the time goes in v1:
time: 666 us; the launch traced here: 665 us
  local copies, waits for them, and re-layouts  523 us (79%)
  blocking collectives  89.6 us (13%)
  starting transfers between devices  19.2 us (3%)
  matrix products  13.1 us (2%)
  other arithmetic  12.5 us (2%)
    gather x29, local copies, waits for them, and re-layouts, select_rows(): return jnp.take_along_axis(shaped, picker, axis=1)[:, 0]  485 us
    psum x5, blocking collectives, one_axis_at_a_time(): array = lax.psum(array, axis)  43.5 us
    all_gather x1, blocking collectives, sent_together(): filled = lax.all_gather(both, axis, axis=dim, tiled=True)  23.6 us
    all_gather x1, blocking collectives, per_device(): lax.all_gather(mid_values, GROUP, axis=0, tiled=True)  22.6 us
    broadcast_in_dim x38, local copies, waits for them, and re-layouts, place_rows(): jnp.where(marked, source[:, None], jnp.asarray(filler, source.dtype))  13.5 us
  transfers between devices with their start and end apart: 3, of which 1 were waited for; matrix products, arithmetic and copies ran while one was open for 13% of the time, Pallas kernels for 0%

profile of v1, /device:TPU:8, one launch (start us, length us, event | category | flops | bytes accessed | tf_op | source)
XLA Modules:
  0.0 665.1 jit_solution(3353676060443782736)
XLA Ops:
  3.5 105.5 %gather_fusion = bf16[10240]{0:T(1024)(128)(2,1)S(1)} fusion(bf16[32,8,5,64]{3,2,1,0:T(8,128)(2,1)S(1)} %reshape_reshape_squeeze.24, s32[10240]{0:T(1024)S(1)} %reshape.1156), kind=kCustom, calls=%fused_computation.clone | custom fusion | bytes 204800 | tf_op jit(solution)/shard_map/jit(take_along_axis)/gather | solution.py:54
  109.5 105.5 %gather_fusion.1 = bf16[10240]{0:T(1024)(128)(2,1)S(1)} fusion(bf16[32,8,5,64]{3,2,1,0:T(8,128)(2,1)S(1)} %reshape_reshape_squeeze.25, s32[10240]{0:T(1024)S(1)} %reshape.1156), kind=kCustom, calls=%fused_computation.4.clone | custom fusion | bytes 204800 | tf_op jit(solution)/shard_map/jit(take_along_axis)/gather | solution.py:54
  215.5 105.5 %gather_fusion.5 = bf16[10240]{0:T(1024)(128)(2,1)S(1)} fusion(bf16[32,8,5,64]{3,2,1,0:T(8,128)(2,1)S(1)} %reshape_reshape_squeeze.29, s32[10240]{0:T(1024)S(1)} %reshape.1156), kind=kCustom, calls=%fused_computation.5.clone | custom fusion | bytes 204800 | tf_op jit(solution)/shard_map/jit(take_along_axis)/gather | solution.py:54
  321.5 105.5 %gather_fusion.7 = bf16[10240]{0:T(1024)(128)(2,1)S(1)} fusion(bf16[32,8,5,64]{3,2,1,0:T(8,128)(2,1)S(1)} %reshape_reshape_squeeze.30, s32[10240]{0:T(1024)S(1)} %reshape.1156), kind=kCustom, calls=%fused_computation.6.clone | custom fusion | bytes 204800 | tf_op jit(solution)/shard_map/jit(take_along_axis)/gather | solution.py:54
  428.1 1.1 reshape.1226
  429.2 7.4 %all-to-all-start = ((bf16[16,2,5120]{2,1,0:T(2,128)(2,1)}), bf16[16,2,5120]{2,1,0:T(2,128)(2,1)S(1)}, u32[]{:S(2)}, u32[]{:S(2)}) async-start(bf16[16,2,5120]{2,1,0:T(2,128)(2,1)} %reshape.1226), calls=%async_computation | async-start | bytes 655360 | tf_op jit(solution)/shard_map/all_to_all | solution.py:191
  438.6 13.7 %gather_fusion.2 = bf16[1280]{0:T(1024)(128)(2,1)S(1)} fusion(bf16[4,64,5,64]{1,0,3,2:T(4,128)(2,1)S(1)} %reshape_reshape_squeeze.26, s32[1280]{0:T(1024)S(1)} %reshape.1168), kind=kCustom, calls=%fused_computation.1.clone | custom fusion | bytes 25600 | tf_op jit(solution)/shard_map/jit(take_along_axis)/gather | solution.py:54
  452.4 13.7 %gather_fusion.3 = bf16[1280]{0:T(1024)(128)(2,1)S(1)} fusion(bf16[4,64,5,64]{1,0,3,2:T(4,128)(2,1)S(1)} %reshape_reshape_squeeze.27, s32[1280]{0:T(1024)S(1)} %reshape.1168), kind=kCustom, calls=%fused_computation.7.clone | custom fusion | bytes 25600 | tf_op jit(solution)/shard_map/jit(take_along_axis)/gather | solution.py:54
  466.2 13.7 %gather_fusion.4 = bf16[1280]{0:T(1024)(128)(2,1)S(1)} fusion(bf16[4,64,5,64]{1,0,3,2:T(4,128)(2,1)S(1)} %reshape_reshape_squeeze.28, s32[1280]{0:T(1024)S(1)} %reshape.1168), kind=kCustom, calls=%fused_computation.8.clone | custom fusion | bytes 25600 | tf_op jit(solution)/shard_map/jit(take_along_axis)/gather | solution.py:54
  479.9 13.7 %gather_fusion.10 = bf16[1280]{0:T(1024)(128)(2,1)S(1)} fusion(bf16[4,64,5,64]{1,0,3,2:T(4,128)(2,1)S(1)} %reshape_reshape_squeeze.31, s32[1280]{0:T(1024)S(1)} %reshape.1168), kind=kCustom, calls=%fused_computation.9.clone | custom fusion | bytes 25600 | tf_op jit(solution)/shard_map/jit(take_along_axis)/gather | solution.py:54
  494.4 23.6 %all_gather.6 = bf16[64,10,64]{2,1,0:T(8,128)(2,1)S(1)} all-gather(bf16[4,10,64]{2,1,0:T(8,128)(2,1)S(1)} %pad_maximum_fusion.3), channel_id=1, replica_groups=mesh['dp'=2,'group_0'=4,'group_1'=4,'seq_0'=4,'seq_1'=2] {'group_0','gro..., dimensions={0}, use_global_device_ids=true | all-gather | bytes 87040 | tf_op jit(solution)/shard_map/all_gather | solution.py:19
  519.3 1.1 broadcast_in_dim.438
  525.8 0.9 copy.305
  528.9 0.8 copy.304
  530.6 22.6 %all-gather = bf16[512,1,5,64]{3,0,2,1:T(8,128)(2,1)S(1)} all-gather(bf16[32,1,5,64]{3,0,2,1:T(8,128)(2,1)S(1)} %copy.297), channel_id=2, replica_groups=mesh['dp'=2,'group_0'=4,'group_1'=4,'seq_0'=4,'seq_1'=2] {'group_0','gro..., dimensions={0}, use_global_device_ids=true | all-gather | bytes 348160 | tf_op jit(solution)/shard_map/all_gather | solution.py:193
  554.4 1.2 select_reduce_fusion.1
  556.9 1.4 subtract_exponential_fusion
  559.2 1.0 copy.307
  560.3 1.5 fusion.33
  562.0 0.8 multiply_reduce_fusion.2
  563.9 2.2 gather_fusion.6
  566.3 2.7 gather_fusion.8
  570.3 0.9 convolution_bitcast_fusion.5
  571.5 0.9 gather_fusion.9
  572.6 0.9 gather_fusion.11
  573.8 0.9 fusion.18
  574.8 0.9 fusion.17
  576.8 0.9 convolution_bitcast_fusion.3
  577.7 0.8 fusion.119
  580.4 1.7 reshape.1230
  583.2 6.0 all-to-all-start.2
  593.1 0.8 copy.311
  594.2 0.9 copy.306
  595.2 0.9 copy.301
  596.2 1.0 broadcast_in_dim.429
  597.2 1.8 fusion.29
  599.2 10.1 %psum.35 = f32[3,40]{1,0:T(4,128)S(1)} all-reduce(f32[3,40]{1,0:T(4,128)S(1)} %dynamic_update_slice.3), channel_id=1, replica_groups=mesh['dp'=2,'group_0'=4,'group_1'=4,'seq_0'=4,'seq_1'=2] {'dp'}, use_global_device_ids=true, to_apply=%region_17.22 | all-reduce | flops 120 | bytes 960 | tf_op jit(solution)/shard_map/psum | solution.py:25
  609.3 10.4 %psum.36 = f32[3,40]{1,0:T(4,128)S(1)} all-reduce(f32[3,40]{1,0:T(4,128)S(1)} %psum.35), channel_id=1, replica_groups=mesh['dp'=2,'group_0'=4,'group_1'=4,'seq_0'=4,'seq_1'=2] {'group_0'}, use_global_device_ids=true, to_apply=%region_18.23 | all-reduce | flops 120 | bytes 960 | tf_op jit(solution)/shard_map/psum | solution.py:25
  619.7 8.8 %psum.37 = f32[3,40]{1,0:T(4,128)S(1)} all-reduce(f32[3,40]{1,0:T(4,128)S(1)} %psum.36), channel_id=1, replica_groups=mesh['dp'=2,'group_0'=4,'group_1'=4,'seq_0'=4,'seq_1'=2] {'group_1'}, use_global_device_ids=true, to_apply=%region_19.24 | all-reduce | flops 120 | bytes 960 | tf_op jit(solution)/shard_map/psum | solution.py:25
  628.5 11.8 %psum.38 = f32[3,40]{1,0:T(4,128)S(1)} all-reduce(f32[3,40]{1,0:T(4,128)S(1)} %psum.37), channel_id=1, replica_groups=mesh['dp'=2,'group_0'=4,'group_1'=4,'seq_0'=4,'seq_1'=2] {'seq_0'}, use_global_device_ids=true, to_apply=%region_20.25 | all-reduce | flops 120 | bytes 960 | tf_op jit(solution)/shard_map/psum | solution.py:25
  640.3 2.5 psum.39
  642.7 5.8 all-to-all-start.1
  650.7 1.0 convolution_bitcast_fusion.2
  651.7 1.0 reshape.1229
  653.4 1.1 broadcast_in_dim.461
  655.4 5.4 all-to-all-done.1
  663.1 1.0 fusion.14
  664.2 0.9 fusion.15
  (405 shorter events, 38.3 us)
Async XLA Ops:
  1.3 437.1 %copy-start.84 = (s32[5]{0:T(128)}, s32[5]{0:T(128)S(1)}, u32[]{:S(2)}) copy-start(s32[5]{0:T(128)S(1)} %broadcast_add_fusion.1) | copy-start | bytes 64
  2.0 436.4 %copy-start.86 = (pred[5]{0:T(512)(128)(4,1)}, pred[5]{0:T(512)(128)(4,1)S(1)}, u32[]{:S(2)}) copy-start(pred[5]{0:T(512)(128)(4,1)S(1)} %broadcast_compare_fusion.1) | copy-start | bytes 19
  3.4 105.6 %copy-start = (bf16[1,256,320]{1,2,0:T(8,128)(2,1)S(1)}, bf16[1,256,320]{1,2,0:T(8,128)(2,1)}, u32[]{:S(2)}) copy-start(bf16[1,256,320]{1,2,0:T(8,128)(2,1)} %param.16) | copy-start | bytes 491524
  109.5 105.6 %copy-start.4 = (bf16[1,256,320]{1,2,0:T(8,128)(2,1)S(1)}, bf16[1,256,320]{1,2,0:T(8,128)(2,1)}, u32[]{:S(2)}) copy-start(bf16[1,256,320]{1,2,0:T(8,128)(2,1)} %param.17) | copy-start | bytes 491524
  215.5 105.6 %copy-start.3 = (bf16[1,256,320]{1,2,0:T(8,128)(2,1)S(1)}, bf16[1,256,320]{1,2,0:T(8,128)(2,1)}, u32[]{:S(2)}) copy-start(bf16[1,256,320]{1,2,0:T(8,128)(2,1)} %param.18) | copy-start | bytes 491524
  321.5 105.6 %copy-start.82 = (s32[5]{0:T(128)S(1)}, s32[5]{0:T(128)}, u32[]{:S(2)}) copy-start(s32[5]{0:T(128)} %param.20) | copy-start | bytes 64
  427.9 8.6 %copy-start.88 = (s32[5]{0:T(128)S(1)}, s32[5]{0:T(128)}, u32[]{:S(2)}) copy-start(s32[5]{0:T(128)} %param.21) | copy-start | bytes 64
  429.2 124.7 %all-to-all-start = ((bf16[16,2,5120]{2,1,0:T(2,128)(2,1)}), bf16[16,2,5120]{2,1,0:T(2,128)(2,1)S(1)}, u32[]{:S(2)}, u32[]{:S(2)}) async-start(bf16[16,2,5120]{2,1,0:T(2,128)(2,1)} %reshape.1226), calls=%async_computation | async-start | bytes 655360 | tf_op jit(solution)/shard_map/all_to_all | solution.py:191
  436.6 57.1 %copy-start.90 = (s32[5]{0:T(128)}, s32[5]{0:T(128)S(1)}, u32[]{:S(2)}) copy-start(s32[5]{0:T(128)S(1)} %broadcast_add_fusion) | copy-start | bytes 64
  436.6 57.1 %copy-start.92 = (pred[5]{0:T(512)(128)(4,1)}, pred[5]{0:T(512)(128)(4,1)S(1)}, u32[]{:S(2)}) copy-start(pred[5]{0:T(512)(128)(4,1)S(1)} %broadcast_compare_fusion) | copy-start | bytes 19
  437.5 85.0 %copy-start.14 = (bf16[1,128,320]{1,2,0:T(8,128)(2,1)}, bf16[1,128,320]{1,2,0:T(8,128)(2,1)S(1)}, u32[]{:S(2)}) copy-start(bf16[1,128,320]{1,2,0:T(8,128)(2,1)S(1)} %get-tuple-element.51) | copy-start | bytes 245764
  437.5 90.4 %copy-start.33 = (pred[128,128]{0,1:T(8,128)(4,1)}, pred[128,128]{0,1:T(8,128)(4,1)S(1)}, u32[]{:S(2)}) copy-start(pred[128,128]{0,1:T(8,128)(4,1)S(1)} %iota_compare_fusion.2) | copy-start | bytes 49156
  437.5 85.0 %copy-start.16 = (bf16[1,128,320]{1,2,0:T(8,128)(2,1)}, bf16[1,128,320]{1,2,0:T(8,128)(2,1)S(1)}, u32[]{:S(2)}) copy-start(bf16[1,128,320]{1,2,0:T(8,128)(2,1)S(1)} %slice.66) | copy-start | bytes 245764
  437.7 85.9 %copy-start.94 = (pred[8,5]{0,1:T(8,128)(4,1)}, pred[8,5]{0,1:T(8,128)(4,1)S(1)}, u32[]{:S(2)}) copy-start(pred[8,5]{0,1:T(8,128)(4,1)S(1)} %iota_compare_fusion.4) | copy-start | bytes 124
  437.7 90.2 %copy-start.27 = (bf16[1,128,320]{1,2,0:T(8,128)(2,1)}, bf16[1,128,320]{1,2,0:T(8,128)(2,1)S(1)}, u32[]{:S(2)}) copy-start(bf16[1,128,320]{1,2,0:T(8,128)(2,1)S(1)} %slice.73) | copy-start | bytes 245764
  438.3 90.6 %copy-start.43 = (pred[256,5]{0,1:T(8,128)(4,1)}, pred[256,5]{0,1:T(8,128)(4,1)S(1)}, u32[]{:S(2)}) copy-start(pred[256,5]{0,1:T(8,128)(4,1)S(1)} %broadcast_in_dim.420) | copy-start | bytes 3844
  494.4 26.1 %copy-start.73 = (bf16[4,5,64]{2,1,0:T(8,128)(2,1)}, bf16[4,5,64]{2,1,0:T(8,128)(2,1)S(1)}, u32[]{:S(2)}) copy-start(bf16[4,5,64]{2,1,0:T(8,128)(2,1)S(1)} %get-tuple-element.78) | copy-start | bytes 7684
  518.5 5.2 copy-start.62
  521.8 5.0 copy-start.20
  522.5 33.6 %copy-start.39 = (f32[5,128]{1,0:T(8,128)}, f32[5,128]{1,0:T(8,128)S(1)}, u32[]{:S(2)}) copy-start(f32[5,128]{1,0:T(8,128)S(1)} %log_add_fusion.6) | copy-start | bytes 7684
  522.8 53.7 %copy-start.1 = (f32[5,128,128]{1,2,0:T(8,128)}, f32[5,128,128]{1,2,0:T(8,128)S(1)}, u32[]{:S(2)}) copy-start(f32[5,128,128]{1,2,0:T(8,128)S(1)} %get-tuple-element.86) | copy-start | bytes 983044
  522.9 33.2 %copy-start.41 = (f32[5,128]{1,0:T(8,128)}, f32[5,128]{1,0:T(8,128)S(1)}, u32[]{:S(2)}) copy-start(f32[5,128]{1,0:T(8,128)S(1)} %log_add_fusion.7) | copy-start | bytes 7684
  523.7 6.1 copy-start.50
  527.1 3.5 copy-start.7
  528.1 26.2 %copy-start.8 = (f32[5,128,64]{1,2,0:T(8,128)}, f32[5,128,64]{1,2,0:T(8,128)S(1)}, u32[]{:S(2)}) copy-start(f32[5,128,64]{1,2,0:T(8,128)S(1)} %fusion.47) | copy-start | bytes 491524
  560.3 3.5 copy-start.61
  560.3 3.5 copy-start.67
  560.3 3.5 copy-start.76
  560.3 3.5 copy-start.95
  563.7 12.8 %copy-start.100 = (f32[5,128]{1,0:T(8,128)}, f32[5,128]{1,0:T(8,128)S(1)}, u32[]{:S(2)}) copy-start(f32[5,128]{1,0:T(8,128)S(1)} %get-tuple-element.88) | copy-start | bytes 7684
  566.2 2.9 copy-start.83
  566.2 2.9 copy-start.85
  566.2 2.9 copy-start.87
  566.3 3.0 copy-start.26
  572.5 3.3 copy-start.36
  572.6 3.9 copy-start.28
  572.6 3.9 copy-start.34
  572.6 3.9 copy-start.48
  572.6 4.2 copy-start.15
  573.5 4.2 copy-start.17
  573.5 5.0 copy-start.13
  580.4 8.9 %copy-start.29 = (f32[32,5,64]{2,0,1:T(8,128)S(1)}, f32[32,5,64]{2,0,1:T(8,128)}, u32[]{:S(2)}) copy-start(f32[32,5,64]{2,0,1:T(8,128)} %convolution_bitcast_fusion.5) | copy-start | bytes 122884
  583.2 59.5 %all-to-all-start.2 = ((bf16[16,2,1280]{2,1,0:T(2,128)(2,1)}), bf16[16,2,1280]{2,1,0:T(2,128)(2,1)}, u32[]{:S(2)}, u32[]{:S(2)}) async-start(bf16[16,2,1280]{2,1,0:T(2,128)(2,1)} %reshape.1228), calls=%async_computation.2 | async-start | bytes 163840 | tf_op jit(solution)/shard_map/all_to_all | solution.py:36
  599.0 51.7 %copy-start.2 = (f32[5,128,128]{1,2,0:T(8,128)S(1)}, f32[5,128,128]{1,2,0:T(8,128)}, u32[]{:S(2)}) copy-start(f32[5,128,128]{1,2,0:T(8,128)} %copy-done.1) | copy-start | bytes 983044
  599.0 51.7 %copy-start.49 = (bf16[1,128,320]{1,2,0:T(8,128)(2,1)S(1)}, bf16[1,128,320]{1,2,0:T(8,128)(2,1)}, u32[]{:S(2)}) copy-start(bf16[1,128,320]{1,2,0:T(8,128)(2,1)} %get-tuple-element.49) | copy-start | bytes 245764
  599.0 51.7 %copy-start.80 = (f32[5]{0:T(128)S(1)}, f32[5]{0:T(128)}, u32[]{:S(2)}) copy-start(f32[5]{0:T(128)} %get-tuple-element.64) | copy-start | bytes 64
  599.0 51.7 %copy-start.101 = (f32[5,128]{1,0:T(8,128)S(1)}, f32[5,128]{1,0:T(8,128)}, u32[]{:S(2)}) copy-start(f32[5,128]{1,0:T(8,128)} %copy-done.100) | copy-start | bytes 7684
  642.7 18.1 %all-to-all-start.1 = ((bf16[16,2,10240]{2,1,0:T(2,128)(2,1)}), bf16[16,2,10240]{2,1,0:T(2,128)(2,1)S(1)}, u32[]{:S(2)}, u32[]{:S(2)}) async-start(bf16[16,2,10240]{2,1,0:T(2,128)(2,1)} %reshape.1230), calls=%async_computation.1 | async-start | bytes 1310720 | tf_op jit(solution)/shard_map/all_to_all | solution.py:36
  (65 other events, 104.8 us)
